TPU v7x, 32 devices: a whole 2x2x4 slice. The times are simulated.
32 devices in a mesh: replica: 16 (over z, y, core), model: 2 (over x).
Axes of the slice: x: 2, y: 2, z: 4, core: 2. Of those that a mesh axis runs over, the one named last changes fastest.
Arguments:
- layer_grads: bfloat16 [16, 2, 4096, 1024], P('replica', None, 'model'), may hold values from -6 to 6
- last_basis: float32 [2, 1024, 32], replicated, may hold values from -6 to 6
- layer_weights: float32 [2, 4096, 1024], P(None, 'model', 'replica'), may hold values from -0.1875 to 0.1875
- momentum: float32 [2, 4096, 1024], P(None, 'model', 'replica'), may hold values from -0.3125 to 0.3125
Outputs:
- new_weights: float32 [2, 4096, 1024], P(None, 'model', 'replica')
- new_basis: float32 [2, 1024, 32], replicated
- new_momentum: float32 [2, 4096, 1024], P(None, 'model', 'replica')
All inputs are finite; a program needn't handle non-finite values.
Results may differ from a plain program's by a relative error of at most 0.0029.
Values sent between devices are 32-bit elements; how exact they have to be, the bound alone decides.
A program may use at most 64 MiB of HBM per device.

v0:
```python
import jax
import jax.numpy as jnp
from jax import lax
from jax.sharding import PartitionSpec as P

RANK = 32


def shards(layer_grads, last_basis, layer_weights, momentum):
    own_grads = layer_grads[0]
    part_left = jnp.einsum(
        "liw,lwr->lir",
        own_grads,
        last_basis.astype(jnp.bfloat16),
        preferred_element_type=jnp.float32,
    )
    shares = lax.psum_scatter(part_left, "replica", scatter_dimension=1, tiled=True)
    left = lax.all_gather(shares, "replica", axis=1, tiled=True)
    part_gram = jnp.einsum("lir,lis->lrs", left, left, precision=lax.Precision.HIGHEST)
    small_left = left.astype(jnp.bfloat16)
    gram = lax.psum(part_gram, "model")
    part_right = jnp.einsum(
        "liw,lir->lwr", own_grads, small_left, preferred_element_type=jnp.float32
    )
    right = lax.psum(part_right, ("replica", "model"))
    gram = gram + 0.001 * jnp.mean(jnp.diagonal(gram, axis1=1, axis2=2), axis=1)[
        :, None, None
    ] * jnp.eye(RANK, dtype=jnp.float32)
    place = lax.axis_index("replica") * layer_weights.shape[2]
    own_right = lax.dynamic_slice_in_dim(right, place, layer_weights.shape[2], axis=1)
    root = jnp.linalg.cholesky(gram)
    half = lax.linalg.triangular_solve(
        root, jnp.swapaxes(own_right, 1, 2), left_side=True, lower=True
    )
    mixed = lax.linalg.triangular_solve(root, half, left_side=True, lower=True, transpose_a=True)
    change = jnp.einsum(
        "lir,lrw->liw", left, mixed, precision=lax.Precision.HIGHEST
    ) / lax.axis_size("replica")
    new_momentum = 0.9 * momentum + change
    new_weights = layer_weights - 0.02 * new_momentum
    new_basis = right * lax.rsqrt(jnp.mean(right * right, axis=(1, 2), keepdims=True) + 1e-12)
    return (new_weights, new_basis, new_momentum)


def solution(mesh):
    in_specs = (
        P("replica", None, "model", None),
        P(),
        P(None, "model", "replica"),
        P(None, "model", "replica"),
    )
    out_specs = (P(None, "model", "replica"), P(), P(None, "model", "replica"))
    return jax.shard_map(shards, mesh=mesh, in_specs=in_specs, out_specs=out_specs, check_vma=False)
```

profile of v0, /device:TPU:1, one launch (start us, length us, event | category | flops | bytes accessed | tf_op | source)
XLA Modules:
  0.0 244.1 jit_solution(10136461796317535133)
XLA Ops:
  7.2 0.0 reduce-scatter.2.cloned.1.call-start
  7.2 6.7 %fusion.2 = f32[2,2048,32]{1,2,0:T(8,128)} fusion(bf16[1,2,2048,1024]{3,2,1,0:T(8,128)(2,1)} %param.4, f32[2,1024,32]{1,2,0:T(8,128)} %param.5), kind=kOutput, calls=%fused_computation.3 | convolution fusion | flops 268500992 | bytes 9175040 | tf_op jit(solution)/shard_map/liw,lwr->lir/dot_general | solution.py:11
  14.0 0.0 all-reduce.2.cloned.1.call-start
  14.0 0.1 copy.13
  14.2 56.3 %reduce-scatter.2.cloned.1.call-done = f32[2,128,32]{1,2,0:T(8,128)} async-done(((f32[2,2048,32]{1,2,0:T(8,128)}), f32[2,128,32]{1,2,0:T(8,128)}) %reduce-scatter.2.cloned.1.call-update) | async-done | bytes 32784 | tf_op jit(solution)/shard_map/reduce_scatter | solution.py:17
  70.5 23.5 %all_gather.3 = f32[2,2048,32]{1,2,0:T(8,128)S(1)} all-gather(f32[2,128,32]{1,2,0:T(8,128)} %reduce-scatter.2.cloned.1.call-done), channel_id=1, replica_groups=mesh['replica'=16,'model'=2] {'replica'}, dimensions={1}, use_global_device_ids=true | all-gather | bytes 557056 | tf_op jit(solution)/shard_map/all_gather | solution.py:18
  94.0 0.6 fusion.18
  94.6 5.8 %fusion.5 = f32[2,1024,32]{1,2,0:T(8,128)} fusion(bf16[1,2,2048,1024]{3,2,1,0:T(8,128)(2,1)} %param.4, f32[2,2048,32]{1,2,0:T(8,128)S(1)} %all_gather.3), kind=kOutput, calls=%fused_computation.7 | convolution fusion | flops 268566528 | bytes 9175040 | tf_op jit(solution)/shard_map/liw,lir->lwr/dot_general | solution.py:22
  100.4 6.3 %psum.14 = f32[2,32,32]{1,2,0:T(8,128)S(1)} all-reduce(f32[2,32,32]{1,2,0:T(8,128)S(1)} %fusion.18), channel_id=1, replica_groups=mesh['replica'=16,'model'=2] {'model'}, use_global_device_ids=true, to_apply=%region_1.0 | all-reduce | flops 2048 | bytes 16384 | tf_op jit(solution)/shard_map/psum | solution.py:21
  106.7 0.6 copy.12
  107.2 0.7 gather_fusion
  108.0 0.1 multiply_add_fusion
  108.1 0.1 copy.14
  108.1 0.1 fusion.14
  108.2 5.9 %custom-call.9 = f32[2,32,32]{2,1,0:T(8,128)S(1)} custom-call(f32[2,32,32]{2,1,0:T(8,128)S(1)} %fusion.14), custom_call_target="Cholesky" | custom-call | tf_op jit(solution)/shard_map/jit(cholesky)/cholesky | solution.py:31
  114.1 0.1 compare_reduce_fusion
  114.2 0.1 select_bitcast_fusion
  114.3 4.9 %custom-call.10 = f32[2,1,32,32]{2,3,1,0:T(8,128)S(1)} custom-call(f32[2,1,32,32]{3,2,1,0:T(8,128)S(1)} %select_bitcast_fusion), custom_call_target="InvertDiagBlocksLowerTriangular" | custom-call | tf_op jit(solution)/shard_map/triangular_solve | solution.py:35
  119.2 111.5 %all-reduce.2.cloned.1.call-done = f32[2,1024,32]{1,2,0:T(8,128)} async-done(((f32[2,1024,32]{1,2,0:T(8,128)}), f32[2,1024,32]{1,2,0:T(8,128)}) %all-reduce.2.cloned.1.call-update) | async-done | bytes 262160 | tf_op jit(solution)/shard_map/psum | solution.py:25
  230.7 1.1 multiply_reduce_fusion
  231.8 1.0 fusion.12
  232.8 0.2 fusion.10
  233.0 2.5 %multiply_subtract_fusion = (f32[2,2048,64]{1,2,0:T(8,128)}, f32[2,2048,64]{1,2,0:T(8,128)}) fusion(f32[2,2048,64]{1,2,0:T(8,128)S(1)} %copy-done, f32[2,2048,32]{1,2,0:T(8,128)S(1)} %all_gather.3, f32[2,32,64]{2,1,0:T(8,128)S(1)} %fusion.10, f32[2,2048,64]{1,2,0:T(8,128)S(1)} %copy-done.1), kind=kOutput, calls=%fused_computation.8 | convolution fusion | flops 101974016 | bytes 4734976 | tf_op jit(solution)/shard_map/lir,lrw->liw/dot_general | solution.py:36
  235.5 1.7 broadcast_multiply_fusion
  (14 shorter events, 0.1 us)
Async XLA Ops:
  7.2 63.3 %reduce-scatter.2.cloned.1.call-start = ((), (), s32[]{:S(2)}) async-start(), calls=%async_computation.1 | async-start | bytes 557056 | tf_op jit(solution)/shard_map/reduce_scatter | solution.py:17
  14.0 216.7 %all-reduce.2.cloned.1.call-start = ((), (), s32[]{:S(2)}) async-start(), calls=%async_computation.2 | async-start | bytes 524288 | tf_op jit(solution)/shard_map/psum | solution.py:25
  94.5 138.4 %copy-start = (f32[2,2048,64]{1,2,0:T(8,128)S(1)}, f32[2,2048,64]{1,2,0:T(8,128)}, u32[]{:S(2)}) copy-start(f32[2,2048,64]{1,2,0:T(8,128)} %param.6) | copy-start | bytes 3145732
  94.6 138.4 %copy-start.1 = (f32[2,2048,64]{1,2,0:T(8,128)S(1)}, f32[2,2048,64]{1,2,0:T(8,128)}, u32[]{:S(2)}) copy-start(f32[2,2048,64]{1,2,0:T(8,128)} %param.7) | copy-start | bytes 3145732
Sparse Core Ops, SparseCore 0:
  14.1 56.3 reduce-scatter.1
  106.8 123.8 all-reduce.1
where the time goes:
time: 246 us; the launch traced here: 244 us
  waiting for transfers between devices  168 us (68%)
  blocking collectives  29.8 us (12%)
  matrix products  16.8 us (7%)
  between operations  14.1 us (6%)
  other arithmetic  14 us (6%)
    psum x1, waiting for transfers between devices, shards(): right = lax.psum(part_right, ('replica', 'model'))  111 us
    reduce_scatter x1, waiting for transfers between devices, shards(): lax.psum_scatter(part_left, 'replica', scatter_dimension=1, tiled=True)  56.3 us
    all_gather x1, blocking collectives, shards(): left = lax.all_gather(shares, 'replica', axis=1, tiled=True)  23.5 us
    dot_general x1, matrix products, shards(): jnp.einsum('liw,lwr->lir', own_grads, last_basis.astype(jnp.bfloat16), pr...  6.75 us
    psum x1, blocking collectives, shards(): gram = lax.psum(part_gram, 'model')  6.3 us
    another operation x4, other arithmetic, shards(): root = jnp.linalg.cholesky(gram)  6.01 us
    dot_general x1, matrix products, shards(): jnp.einsum('liw,lir->lwr', own_grads, small_left, preferred_element_type=...  5.78 us
    another operation x3, other arithmetic, shards(): lax.linalg.triangular_solve(root, half, left_side=True, lower=True, trans...  5 us
  transfers between devices with their start and end apart: 2, of which 2 were waited for; matrix products, arithmetic and copies ran while one was open for 5% of the time, Pallas kernels for 0%

commit v1 on v0

v1 whole, which is shorter than its diff:
```python
import functools

import jax
import jax.numpy as jnp
from jax import lax
from jax.experimental import pallas as pl
from jax.experimental.pallas import tpu as pltpu
from jax.sharding import PartitionSpec as P

LANES = 128
F32 = jnp.float32
BF16 = jnp.bfloat16
NT = (((1,), (1,)), ((), ()))


def split(value):
    high = value.astype(BF16)
    return high, (value - high.astype(F32)).astype(BF16)


def invert(a, rank, first):
    lane = lax.broadcasted_iota(jnp.int32, a.shape, 1)
    sub = lax.broadcasted_iota(jnp.int32, a.shape, 0)
    for p in range(rank):
        at = first + p
        row = a[p : p + 1, :]
        col = a[:, at : at + 1]
        inverse = 1.0 / a[p : p + 1, at : at + 1]
        row = jnp.where(lane[:1] == at, 1.0, row) * inverse
        a = jnp.where(sub == p, row, jnp.where(lane == at, 0.0, a) - col * row)
    return a


def kernel(
    n, m, grads, basis, weights, momentum, out_w, out_b, out_m,
    g, b, w, mom, stack, part, from_core, summed, arrived, left,
    r_part, r_core, r_sum, r_arrived, r_model, right, gram, basis_out,
    load_sem, core_s, core_r, rs_s, rs_r, ag_s, ag_r, fwd_s, fwd_r,
    mod_s, mod_r,
):
    layers, rows, width = g.shape
    rank = b.shape[2]
    pair = layers * rank
    q = n // 2
    half = rows // 2
    blocks = half // LANES
    wc = width // n
    me = lax.axis_index("replica")
    x = lax.axis_index("model")
    c, k = lax.rem(me, 2), me // 2
    o = 1 - c

    def near(d):
        return lax.rem(k + d, q)

    def before(d):
        return lax.rem(k + q - d, q)

    def send(src, dst, s, r, device):
        copy = pltpu.make_async_remote_copy(
            src_ref=src, dst_ref=dst, send_sem=s, recv_sem=r,
            device_id=device, device_id_type=pl.DeviceIdType.MESH,
        )
        copy.start()
        return copy

    partner = {"replica": 2 * k + o}

    def chip(d):
        return {"replica": 2 * near(d) + c}

    def other(d):
        return {"model": lax.rem(x + d, m)}

    def rows_of(h):
        return pl.ds(pl.multiple_of(h * half, half), half)

    load_b = pltpu.make_async_copy(basis, b, load_sem.at[0])
    load_b.start()
    loads = []
    for i, h in enumerate((o, c)):
        for l in range(layers):
            copy = pltpu.make_async_copy(
                grads.at[0, l, rows_of(h)], g.at[l, rows_of(h)],
                load_sem.at[3 + i * layers + l],
            )
            copy.start()
            loads.append(copy)
    load_m = pltpu.make_async_copy(momentum, mom, load_sem.at[1])
    load_w = pltpu.make_async_copy(weights, w, load_sem.at[2])
    load_m.start()
    load_w.start()

    barrier = pltpu.get_barrier_semaphore()
    peers = [partner] + [chip(d) for d in range(1, q)] + [other(d) for d in range(1, m)]
    for device in peers:
        pl.semaphore_signal(
            barrier, inc=1, device_id=device, device_id_type=pl.DeviceIdType.MESH
        )

    load_b.wait()
    turned = [b[l].T.astype(BF16) for l in range(layers)]

    def part_of(h, i):
        for l in range(layers):
            loads[i * layers + l].wait()
            value = lax.dot_general(
                turned[l], g[l, rows_of(h), :], NT, preferred_element_type=F32
            )
            for j in range(blocks):
                at = pl.multiple_of((h * blocks + j) * pair + l * rank, rank)
                part[pl.ds(at, rank), :] = value[:, j * LANES : (j + 1) * LANES]

    waits = []

    def reduce_scatter(source, near_buf, sums, far_buf, phase, mid, mid2):
        size = source.shape[0] // 2
        share = size // q
        mine = pl.ds(pl.multiple_of(c * size, size), size)
        theirs = pl.ds(pl.multiple_of(o * size, size), size)
        core = send(source.at[theirs], near_buf, core_s.at[phase], core_r.at[phase], partner)
        mid()
        core.wait_recv()
        sums[...] = source[mine, :] + near_buf[...]
        copies = []
        for d in range(1, q):
            to = pl.ds(pl.multiple_of(near(d) * share, share), share)
            copies.append(
                send(sums.at[to], far_buf.at[d - 1], rs_s.at[phase, d - 1],
                     rs_r.at[phase, d - 1], chip(d))
            )
        mid2()
        total = sums[pl.ds(pl.multiple_of(k * share, share), share), :]
        for d in range(1, q):
            copies[d - 1].wait_recv()
            total = total + far_buf[d - 1]
        waits.extend([core] + copies)
        return total

    def gather_start(buf, phase):
        share = buf.shape[0] // n
        own = pl.ds(pl.multiple_of((c * q + k) * share, share), share)
        copies = [
            send(buf.at[own], buf.at[own], ag_s.at[phase, d - 1], ag_r.at[phase, d - 1], chip(d))
            for d in range(1, q)
        ]
        forwards = [
            send(buf.at[own], buf.at[own], fwd_s.at[phase, 0], fwd_r.at[phase, 0], partner)
        ]
        return copies, forwards

    def gather_pass(buf, phase, copies, forwards):
        share = buf.shape[0] // n
        for d in range(1, q):
            copies[d - 1].wait_recv()
            at = pl.ds(pl.multiple_of((c * q + before(d)) * share, share), share)
            forwards.append(
                send(buf.at[at], buf.at[at], fwd_s.at[phase, d], fwd_r.at[phase, d], partner)
            )

    def gather_end(copies, forwards):
        for copy in forwards:
            copy.wait_recv()
        waits.extend(copies + forwards)

    part_of(o, 0)
    pl.semaphore_wait(barrier, len(peers))
    share = reduce_scatter(
        part, from_core, summed, arrived, 0, lambda: part_of(c, 1), lambda: None
    )
    size = part.shape[0] // n
    left[pl.ds(pl.multiple_of((c * q + k) * size, size), size), :] = share
    copies, forwards = gather_start(left, 0)
    gather_pass(left, 0, copies, forwards)

    def lefts(h):
        return [
            jnp.concatenate(
                [
                    left[pl.ds(pl.multiple_of((h * blocks + j) * pair + l * rank, rank), rank), :]
                    for j in range(blocks)
                ],
                axis=1,
            )
            for l in range(layers)
        ]

    def right_of(h):
        return [
            jnp.dot(value.astype(BF16), g[l, rows_of(h), :], preferred_element_type=F32)
            for l, value in enumerate(lefts(h))
        ]

    own_right = right_of(c)
    gather_end(copies, forwards)
    own_right = [a + v for a, v in zip(own_right, right_of(o))]
    if layers * wc < LANES:
        r_part[...] = jnp.zeros_like(r_part)
    for idx in range(n):
        at = ((idx % 2) * q + idx // 2) * rank
        for l in range(layers):
            r_part[at : at + rank, l * wc : (l + 1) * wc] = own_right[l][:, idx * wc : (idx + 1) * wc]

    gram_copies = []

    def make_gram():
        total = jnp.zeros((pair, pair), F32)
        for h in range(2):
            both = jnp.concatenate(lefts(h), axis=0)
            total = total + lax.dot_general(
                both, both, NT, precision=lax.Precision.HIGHEST, preferred_element_type=F32
            )
        gram[x] = jnp.concatenate([total, jnp.zeros((pair, LANES - pair), F32)], axis=1)
        for d in range(1, m):
            gram_copies.append(
                send(gram.at[x], gram.at[x], mod_s.at[0, d - 1], mod_r.at[0, d - 1], other(d))
            )

    inverses = []

    def solve():
        for h in range(2):
            for l, value in enumerate(lefts(h)):
                high, low = split(value)
                stack[l, h * half : (h + 1) * half, :] = jnp.concatenate(
                    [high, high, low, low], axis=0
                ).T
        for copy in gram_copies:
            copy.wait_recv()
        total = gram[0]
        for i in range(1, m):
            total = total + gram[i]
        for l in range(layers):
            a = total[l * rank : (l + 1) * rank, :]
            sub = lax.broadcasted_iota(jnp.int32, a.shape, 0)
            lane = lax.broadcasted_iota(jnp.int32, a.shape, 1)
            diagonal = lane == sub + l * rank
            ridge = 0.001 * jnp.sum(jnp.where(diagonal, a, 0.0)) / rank
            a = a + jnp.where(diagonal, ridge, 0.0)
            a = invert(a, rank, l * rank)
            inside = (lane >= l * rank) & (lane < (l + 1) * rank)
            inverses.append(jnp.where(inside, a, 0.0)[:, :pair])

    total = reduce_scatter(r_part, r_core, r_sum, r_arrived, 1, make_gram, solve)
    waits.extend(gram_copies)
    r_model[x] = total
    swaps = [
        send(r_model.at[x], r_model.at[x], mod_s.at[1, d - 1], mod_r.at[1, d - 1], other(d))
        for d in range(1, m)
    ]
    for copy in swaps:
        copy.wait_recv()
    waits.extend(swaps)
    total = r_model[0]
    for i in range(1, m):
        total = total + r_model[i]
    right[pl.ds(pl.multiple_of((c * q + k) * rank, rank), rank), :] = total
    copies, forwards = gather_start(right, 1)

    mixed = jnp.dot(
        jnp.concatenate(inverses, axis=0),
        jnp.concatenate([total] * layers, axis=0),
        precision=lax.Precision.HIGHEST,
        preferred_element_type=F32,
    ) / n
    load_m.wait()
    load_w.wait()
    stores = []
    for l in range(layers):
        high, low = split(mixed[l * rank : (l + 1) * rank, l * wc : (l + 1) * wc])
        change = jnp.dot(
            stack[l], jnp.concatenate([high, low, high, low], axis=0), preferred_element_type=F32
        )
        new_m = 0.9 * mom[l] + change
        mom[l] = new_m
        w[l] = w[l] - 0.02 * new_m
        for src, dst, i in ((mom, out_m, 0), (w, out_w, 1)):
            copy = pltpu.make_async_copy(src.at[l], dst.at[l], load_sem.at[3 + 2 * l + i])
            copy.start()
            stores.append(copy)

    gather_pass(right, 1, copies, forwards)
    gather_end(copies, forwards)
    squares = jnp.zeros((rank, LANES), F32)
    for pos in range(n):
        value = right[pos * rank : (pos + 1) * rank, :]
        squares = squares + value * value
    lane = lax.broadcasted_iota(jnp.int32, squares.shape, 1)
    scales = [
        lax.rsqrt(
            jnp.sum(
                jnp.where((lane >= l * wc) & (lane < (l + 1) * wc), squares, 0.0),
                axis=(0, 1), keepdims=True,
            ) / (width * rank) + 1e-12
        )
        for l in range(layers)
    ]
    for idx in range(n):
        at = ((idx % 2) * q + idx // 2) * rank
        value = right[at : at + rank, :].T
        for l in range(layers):
            basis_out[l, idx * wc : (idx + 1) * wc, :] = value[l * wc : (l + 1) * wc, :] * scales[l]
    copy = pltpu.make_async_copy(basis_out, out_b, load_sem.at[0])
    copy.start()
    stores.append(copy)
    for copy in waits:
        copy.wait_send()
    for copy in stores:
        copy.wait()


def shards(n, m, layer_grads, last_basis, layer_weights, momentum):
    _, layers, rows, width = layer_grads.shape
    rank = last_basis.shape[2]
    pair = layers * rank
    q = n // 2
    tall = rows // LANES * pair
    dma = pltpu.SemaphoreType.DMA
    vmem = pltpu.VMEM
    return pl.pallas_call(
        functools.partial(kernel, n, m),
        out_shape=(
            jax.ShapeDtypeStruct(layer_weights.shape, F32),
            jax.ShapeDtypeStruct(last_basis.shape, F32),
            jax.ShapeDtypeStruct(momentum.shape, F32),
        ),
        in_specs=[pl.BlockSpec(memory_space=pl.ANY)] * 4,
        out_specs=[pl.BlockSpec(memory_space=pl.ANY)] * 3,
        scratch_shapes=[
            vmem((layers, rows, width), BF16),
            vmem(last_basis.shape, F32),
            vmem(layer_weights.shape, F32),
            vmem(momentum.shape, F32),
            vmem((layers, rows, 4 * rank), BF16),
            vmem((tall, LANES), F32),
            vmem((tall // 2, LANES), F32),
            vmem((tall // 2, LANES), F32),
            vmem((q - 1, tall // n, LANES), F32),
            vmem((tall, LANES), F32),
            vmem((n * rank, LANES), F32),
            vmem((q * rank, LANES), F32),
            vmem((q * rank, LANES), F32),
            vmem((q - 1, rank, LANES), F32),
            vmem((m, rank, LANES), F32),
            vmem((n * rank, LANES), F32),
            vmem((m, pair, LANES), F32),
            vmem(last_basis.shape, F32),
            dma((3 + 2 * layers,)),
            dma((2,)), dma((2,)),
            dma((2, q - 1)), dma((2, q - 1)),
            dma((2, q - 1)), dma((2, q - 1)),
            dma((2, q)), dma((2, q)),
            dma((2, m - 1)), dma((2, m - 1)),
        ],
        compiler_params=pltpu.CompilerParams(
            collective_id=0, has_side_effects=True, vmem_limit_bytes=32 * 1024 * 1024
        ),
        name="step",
    )(layer_grads, last_basis, layer_weights, momentum)


def solution(mesh):
    in_specs = (
        P("replica", None, "model", None),
        P(),
        P(None, "model", "replica"),
        P(None, "model", "replica"),
    )
    out_specs = (P(None, "model", "replica"), P(), P(None, "model", "replica"))
    body = functools.partial(shards, mesh.shape["replica"], mesh.shape["model"])
    return jax.shard_map(body, mesh=mesh, in_specs=in_specs, out_specs=out_specs, check_vma=False)
```

time: 246 us -> 63.5 us (0.26)
  waiting for transfers between devices: 168 us -> 0 us
  Pallas kernels: 0 us -> 41.8 us
  blocking collectives: 29.8 us -> 0 us
  local copies, waits for them, and re-layouts: 1.42 us -> 20.8 us
  matrix products: 16.8 us -> 0 us
  other arithmetic: 14 us -> 0 us
  between operations: 14.1 us -> 0.67 us
    psum x1 -> x0, waiting for transfers between devices: 111 us -> none  [shards(): right = lax.psum(part_right, ('replica', 'model'))]
    reduce_scatter x1 -> x0, waiting for transfers between devices: 56.3 us -> none  [shards(): lax.psum_scatter(part_left, 'replica', scatter_dimension=1, tiled=True)]
    pallas_call x0 -> x1, Pallas kernels: none -> 41.8 us  [shards(): pl.pallas_call(functools.partial(kernel, n, m), out_shape=(jax.ShapeDtype...]
    all_gather x1 -> x0, blocking collectives: 23.5 us -> none  [shards(): left = lax.all_gather(shares, 'replica', axis=1, tiled=True)]
    dot_general x4 -> x0, matrix products: 15.6 us -> none  [the longest x1 6.75 us: shards(): jnp.einsum('liw,lwr->lir', own_grads, last_basis.astype(jnp.bfloat16), pr...]
    unnamed x4 -> x17, local copies, waits for them, and re-layouts: 0.02 us -> 14.9 us
    another operation x7 -> x0, other arithmetic: 11 us -> none  [the longest x4 6.01 us: shards(): root = jnp.linalg.cholesky(gram)]
    psum x1 -> x0, blocking collectives: 6.3 us -> none  [shards(): gram = lax.psum(part_gram, 'model')]
  transfers between devices with their start and end apart: 2 -> 0, of which waited for: 2 -> 0; matrix products, arithmetic and copies ran while one was open for 5% -> 0% of each run, Pallas kernels for 0% -> 0%
where the time goes in v1:
time: 63.5 us; the launch traced here: 63.2 us
  Pallas kernels  41.8 us (66%)
  local copies, waits for them, and re-layouts  20.8 us (33%)
  between operations  0.67 us (1%)
    pallas_call x1, Pallas kernels, shards(): pl.pallas_call(functools.partial(kernel, n, m), out_shape=(jax.ShapeDtype...  41.8 us
    unnamed x17, local copies, waits for them, and re-layouts  14.9 us
    pallas_call x3, local copies, waits for them, and re-layouts, shards(): pl.pallas_call(functools.partial(kernel, n, m), out_shape=(jax.ShapeDtype...  5.87 us

profile of v1, /device:TPU:1, one launch (start us, length us, event | category | flops | bytes accessed | tf_op | source)
XLA Modules:
  0.0 63.2 jit_solution(9619761726861851052)
XLA Ops:
  0.6 1.3 %copy.7.basis = f32[2,1024,32]{2,1,0:T(8,128)S(1)} copy(f32[2,1024,32]{1,2,0:T(8,128)} %param.5) | data formatting | bytes 524288 | tf_op args[1]
  1.9 1.8 %copy.8.weights = f32[2,2048,64]{2,1,0:T(8,128)S(1)} copy(f32[2,2048,64]{1,2,0:T(8,128)} %param.6) | data formatting | bytes 2097152 | tf_op args[2]
  3.8 3.2 %copy.9.momentum = f32[2,2048,64]{2,1,0:T(8,128)} copy(f32[2,2048,64]{1,2,0:T(8,128)} %param.7) | data formatting | bytes 2097152 | tf_op args[3]
  6.9 0.0 copy-start
  6.9 3.4 %copy-done = bf16[1,2,2048,1024]{3,2,1,0:T(8,128)(2,1)S(1)} copy-done((bf16[1,2,2048,1024]{3,2,1,0:T(8,128)(2,1)S(1)}, bf16[1,2,2048,1024]{3,2,1,0:T(8,128)(2,1)}, u32[]{:S(2)}) %copy-start) | copy-done | bytes 8388632
  10.3 0.0 copy-start.1
  10.3 1.6 %copy-done.1 = f32[2,2048,64]{2,1,0:T(8,128)S(1)} copy-done((f32[2,2048,64]{2,1,0:T(8,128)S(1)}, f32[2,2048,64]{2,1,0:T(8,128)}, u32[]{:S(2)}) %copy-start.1) | copy-done | bytes 1048600
  11.9 41.8 %step.1 = (f32[2,2048,64]{2,1,0:T(8,128)S(1)}, f32[2,1024,32]{2,1,0:T(8,128)S(1)}, f32[2,2048,64]{2,1,0:T(8,128)S(1)}) custom-call(bf16[1,2,2048,1024]{3,2,1,0:T(8,128)(2,1)S(1)} %copy-done, f32[2,1024,32]{2,1,0:T(8,128)S(1)} %copy.7.basis, f32[2,2048,64]{2,1,0:T(8,128)S(1)} %copy.8.weights, f32[2,2048,64]{2,1,0:T(8,128)S(1)} %copy-done.1), custom_call_target="tpu_custom_call" | custom-call | tf_op jit(solution)/shard_map/step/pallas_call | solution.py:320
  53.7 0.0 copy-start.2
  53.7 1.3 %copy-done.2 = f32[2,2048,64]{2,1,0:T(8,128)} copy-done((f32[2,2048,64]{2,1,0:T(8,128)}, f32[2,2048,64]{2,1,0:T(8,128)S(1)}, u32[]{:S(2)}) %copy-start.2) | copy-done | bytes 1048600
  55.1 0.0 copy-start.4
  55.1 1.3 %copy-done.4 = f32[2,2048,64]{2,1,0:T(8,128)} copy-done((f32[2,2048,64]{2,1,0:T(8,128)}, f32[2,2048,64]{2,1,0:T(8,128)S(1)}, u32[]{:S(2)}) %copy-start.4) | copy-done | bytes 1048600
  56.4 0.0 copy-start.5
  56.4 1.0 %copy-done.5 = f32[2,1024,32]{2,1,0:T(8,128)} copy-done((f32[2,1024,32]{2,1,0:T(8,128)}, f32[2,1024,32]{2,1,0:T(8,128)S(1)}, u32[]{:S(2)}) %copy-start.5) | copy-done | bytes 262168
  57.3 0.0 copy-start.6
  57.4 0.0 copy-start.3
  57.4 3.3 %copy.10 = f32[2,2048,64]{1,2,0:T(8,128)} copy(f32[2,2048,64]{2,1,0:T(8,128)} %copy-done.4) | data formatting | bytes 2097152 | tf_op jit(solution)/shard_map/step/pallas_call | solution.py:320
  60.7 0.0 copy-done.6
  60.7 1.0 %copy.11 = f32[2,1024,32]{1,2,0:T(8,128)} copy(f32[2,1024,32]{2,1,0:T(8,128)S(1)} %copy-done.6) | data formatting | bytes 524288 | tf_op jit(solution)/shard_map/step/pallas_call | solution.py:320
  61.7 0.0 copy-done.3
  61.7 1.6 %copy.12 = f32[2,2048,64]{1,2,0:T(8,128)} copy(f32[2,2048,64]{2,1,0:T(8,128)S(1)} %copy-done.3) | data formatting | bytes 2097152 | tf_op jit(solution)/shard_map/step/pallas_call | solution.py:320
Async XLA Ops:
  6.9 3.4 %copy-start = (bf16[1,2,2048,1024]{3,2,1,0:T(8,128)(2,1)S(1)}, bf16[1,2,2048,1024]{3,2,1,0:T(8,128)(2,1)}, u32[]{:S(2)}) copy-start(bf16[1,2,2048,1024]{3,2,1,0:T(8,128)(2,1)} %grads.1) | copy-start | bytes 25165828
  10.3 1.6 %copy-start.1 = (f32[2,2048,64]{2,1,0:T(8,128)S(1)}, f32[2,2048,64]{2,1,0:T(8,128)}, u32[]{:S(2)}) copy-start(f32[2,2048,64]{2,1,0:T(8,128)} %copy.9.momentum) | copy-start | bytes 3145732
  53.7 1.3 %copy-start.2 = (f32[2,2048,64]{2,1,0:T(8,128)}, f32[2,2048,64]{2,1,0:T(8,128)S(1)}, u32[]{:S(2)}) copy-start(f32[2,2048,64]{2,1,0:T(8,128)S(1)} %get-tuple-element.5) | copy-start | bytes 3145732
  55.1 1.3 %copy-start.4 = (f32[2,2048,64]{2,1,0:T(8,128)}, f32[2,2048,64]{2,1,0:T(8,128)S(1)}, u32[]{:S(2)}) copy-start(f32[2,2048,64]{2,1,0:T(8,128)S(1)} %get-tuple-element.3) | copy-start | bytes 3145732
  56.4 1.0 %copy-start.5 = (f32[2,1024,32]{2,1,0:T(8,128)}, f32[2,1024,32]{2,1,0:T(8,128)S(1)}, u32[]{:S(2)}) copy-start(f32[2,1024,32]{2,1,0:T(8,128)S(1)} %get-tuple-element.4) | copy-start | bytes 786436
  57.3 3.3 %copy-start.6 = (f32[2,1024,32]{2,1,0:T(8,128)S(1)}, f32[2,1024,32]{2,1,0:T(8,128)}, u32[]{:S(2)}) copy-start(f32[2,1024,32]{2,1,0:T(8,128)} %copy-done.5) | copy-start | bytes 786436
  57.4 4.3 %copy-start.3 = (f32[2,2048,64]{2,1,0:T(8,128)S(1)}, f32[2,2048,64]{2,1,0:T(8,128)}, u32[]{:S(2)}) copy-start(f32[2,2048,64]{2,1,0:T(8,128)} %copy-done.2) | copy-start | bytes 3145732

commit v2 on v1

--- a/solution.py
+++ b/solution.py
@@ -8,6 +8,9 @@
 from jax.sharding import PartitionSpec as P
 
 LANES = 128
+MIB = 1024 * 1024
+LIMIT = 32 * MIB
+LIMIT2 = 16 * MIB
 F32 = jnp.float32
 BF16 = jnp.bfloat16
 NT = (((1,), (1,)), ((), ()))
@@ -39,7 +42,7 @@
     mod_s, mod_r,
 ):
     layers, rows, width = g.shape
-    rank = b.shape[2]
+    rank = b.shape[1]
     pair = layers * rank
     q = n // 2
     half = rows // 2
@@ -99,7 +102,7 @@
         )
 
     load_b.wait()
-    turned = [b[l].T.astype(BF16) for l in range(layers)]
+    turned = [b[l].astype(BF16) for l in range(layers)]
 
     def part_of(h, i):
         for l in range(layers):
@@ -222,9 +225,9 @@
         for h in range(2):
             for l, value in enumerate(lefts(h)):
                 high, low = split(value)
-                stack[l, h * half : (h + 1) * half, :] = jnp.concatenate(
+                stack[l, :, h * half : (h + 1) * half] = jnp.concatenate(
                     [high, high, low, low], axis=0
-                ).T
+                )
         for copy in gram_copies:
             copy.wait_recv()
         total = gram[0]
@@ -268,8 +271,9 @@
     stores = []
     for l in range(layers):
         high, low = split(mixed[l * rank : (l + 1) * rank, l * wc : (l + 1) * wc])
-        change = jnp.dot(
-            stack[l], jnp.concatenate([high, low, high, low], axis=0), preferred_element_type=F32
+        change = lax.dot_general(
+            jnp.concatenate([high, low, high, low], axis=0), stack[l],
+            (((0,), (0,)), ((), ())), preferred_element_type=F32,
         )
         new_m = 0.9 * mom[l] + change
         mom[l] = new_m
@@ -297,9 +301,9 @@
     ]
     for idx in range(n):
         at = ((idx % 2) * q + idx // 2) * rank
-        value = right[at : at + rank, :].T
+        value = right[at : at + rank, :]
         for l in range(layers):
-            basis_out[l, idx * wc : (idx + 1) * wc, :] = value[l * wc : (l + 1) * wc, :] * scales[l]
+            basis_out[l, :, idx * wc : (idx + 1) * wc] = value[:, l * wc : (l + 1) * wc] * scales[l]
     copy = pltpu.make_async_copy(basis_out, out_b, load_sem.at[0])
     copy.start()
     stores.append(copy)
@@ -309,29 +313,43 @@
         copy.wait()
 
 
+def write_out(*refs):
+    sems = refs[-1]
+    copies = [
+        pltpu.make_async_copy(refs[i], refs[i + 3], sems.at[i]) for i in range(3)
+    ]
+    for copy in copies:
+        copy.start()
+    for copy in copies:
+        copy.wait()
+
+
 def shards(n, m, layer_grads, last_basis, layer_weights, momentum):
     _, layers, rows, width = layer_grads.shape
-    rank = last_basis.shape[2]
+    last_basis, layer_weights, momentum = (
+        jnp.swapaxes(a, 1, 2) for a in (last_basis, layer_weights, momentum)
+    )
+    rank = last_basis.shape[1]
     pair = layers * rank
     q = n // 2
     tall = rows // LANES * pair
     dma = pltpu.SemaphoreType.DMA
     vmem = pltpu.VMEM
-    return pl.pallas_call(
+    outs = pl.pallas_call(
         functools.partial(kernel, n, m),
         out_shape=(
             jax.ShapeDtypeStruct(layer_weights.shape, F32),
             jax.ShapeDtypeStruct(last_basis.shape, F32),
             jax.ShapeDtypeStruct(momentum.shape, F32),
         ),
-        in_specs=[pl.BlockSpec(memory_space=pl.ANY)] * 4,
+        in_specs=[pl.BlockSpec(memory_space=pltpu.HBM)] * 4,
         out_specs=[pl.BlockSpec(memory_space=pl.ANY)] * 3,
         scratch_shapes=[
             vmem((layers, rows, width), BF16),
             vmem(last_basis.shape, F32),
             vmem(layer_weights.shape, F32),
             vmem(momentum.shape, F32),
-            vmem((layers, rows, 4 * rank), BF16),
+            vmem((layers, 4 * rank, rows), BF16),
             vmem((tall, LANES), F32),
             vmem((tall // 2, LANES), F32),
             vmem((tall // 2, LANES), F32),
@@ -353,10 +371,25 @@
             dma((2, m - 1)), dma((2, m - 1)),
         ],
         compiler_params=pltpu.CompilerParams(
-            collective_id=0, has_side_effects=True, vmem_limit_bytes=32 * 1024 * 1024
+            collective_id=0, has_side_effects=True, vmem_limit_bytes=LIMIT
         ),
         name="step",
-    )(layer_grads, last_basis, layer_weights, momentum)
+    )(
+        *(
+            pltpu.with_memory_space_constraint(a, pltpu.HBM)
+            for a in (layer_grads, last_basis, layer_weights, momentum)
+        )
+    )
+    outs = pl.pallas_call(
+        write_out,
+        out_shape=tuple(jax.ShapeDtypeStruct(a.shape, F32) for a in outs),
+        in_specs=[pl.BlockSpec(memory_space=pl.ANY)] * 3,
+        out_specs=[pl.BlockSpec(memory_space=pltpu.HBM)] * 3,
+        scratch_shapes=[dma((3,))],
+        compiler_params=pltpu.CompilerParams(vmem_limit_bytes=LIMIT2),
+        name="write_out",
+    )(*outs)
+    return tuple(jnp.swapaxes(a, 1, 2) for a in outs)
 
 
 def solution(mesh):

time: 63.5 us -> 42.6 us (0.67)
  local copies, waits for them, and re-layouts: 20.8 us -> 0 us
    unnamed x17 -> x0, local copies, waits for them, and re-layouts: 14.9 us -> none
    pallas_call x3 -> x0, local copies, waits for them, and re-layouts: 5.87 us -> none  [shards(): pl.pallas_call(functools.partial(kernel, n, m), out_shape=(jax.ShapeDtype...]
    pallas_call x0 -> x1, Pallas kernels: none -> 1.43 us  [shards(): pl.pallas_call(write_out, out_shape=tuple((jax.ShapeDtypeStruct(a.shape,...]
    pallas_call x1, Pallas kernels: 41.8 us -> 40.4 us  [shards(): pl.pallas_call(functools.partial(kernel, n, m), out_shape=(jax.ShapeDtype...]
where the time goes in v2:
time: 42.6 us; the launch traced here: 42.5 us
  Pallas kernels  41.9 us (98%)
  between operations  0.64 us (2%)
    pallas_call x1, Pallas kernels, shards(): pl.pallas_call(functools.partial(kernel, n, m), out_shape=(jax.ShapeDtype...  40.4 us
    pallas_call x1, Pallas kernels, shards(): pl.pallas_call(write_out, out_shape=tuple((jax.ShapeDtypeStruct(a.shape,...  1.43 us

profile of v2, /device:TPU:1, one launch (start us, length us, event | category | flops | bytes accessed | tf_op | source)
XLA Modules:
  0.0 42.5 jit_solution(4779969383637861486)
XLA Ops:
  0.6 40.4 %step.1 = (f32[2,64,2048]{2,1,0:T(8,128)S(1)}, f32[2,32,1024]{2,1,0:T(8,128)S(1)}, f32[2,64,2048]{2,1,0:T(8,128)S(1)}) custom-call(bf16[1,2,2048,1024]{3,2,1,0:T(8,128)(2,1)} %grads.1, f32[2,32,1024]{2,1,0:T(8,128)} %bitcast.8, f32[2,64,2048]{2,1,0:T(8,128)} %bitcast.6, f32[2,64,2048]{2,1,0:T(8,128)} %bitcast.7), custom_call_target="tpu_custom_call" | custom-call | tf_op jit(solution)/shard_map/step/pallas_call | solution.py:338
  41.1 1.4 %write_out.1 = (f32[2,64,2048]{2,1,0:T(8,128)}, f32[2,32,1024]{2,1,0:T(8,128)}, f32[2,64,2048]{2,1,0:T(8,128)}) custom-call(f32[2,64,2048]{2,1,0:T(8,128)S(1)} %get-tuple-element.9.refs_0_, f32[2,32,1024]{2,1,0:T(8,128)S(1)} %get-tuple-element.10.refs_1_, f32[2,64,2048]{2,1,0:T(8,128)S(1)} %get-tuple-element.11.refs_2_), custom_call_target="tpu_custom_call" | custom-call | tf_op jit(solution)/shard_map/write_out/pallas_call | solution.py:383

commit v3 on v2

--- a/solution.py
+++ b/solution.py
@@ -44,6 +44,8 @@
     layers, rows, width = g.shape
     rank = b.shape[1]
     pair = layers * rank
+    groups = part.shape[0]
+    deep = layers // groups
     q = n // 2
     half = rows // 2
     blocks = half // LANES
@@ -81,11 +83,10 @@
     load_b = pltpu.make_async_copy(basis, b, load_sem.at[0])
     load_b.start()
     loads = []
-    for i, h in enumerate((o, c)):
-        for l in range(layers):
+    for l in range(layers):
+        for i, h in enumerate((o, c)):
             copy = pltpu.make_async_copy(
-                grads.at[0, l, rows_of(h)], g.at[l, rows_of(h)],
-                load_sem.at[3 + i * layers + l],
+                grads.at[0, l, rows_of(h)], g.at[l, rows_of(h)], load_sem.at[3 + 2 * l + i]
             )
             copy.start()
             loads.append(copy)
@@ -104,25 +105,34 @@
     load_b.wait()
     turned = [b[l].astype(BF16) for l in range(layers)]
 
-    def part_of(h, i):
-        for l in range(layers):
-            loads[i * layers + l].wait()
+    def block_of(h, j, l):
+        at = ((h * blocks + j) * deep + l % deep) * rank
+        return pl.ds(pl.multiple_of(at, rank), rank)
+
+    def part_of(h, i, group):
+        for l in range(group * deep, (group + 1) * deep):
+            loads[2 * l + i].wait()
             value = lax.dot_general(
                 turned[l], g[l, rows_of(h), :], NT, preferred_element_type=F32
             )
             for j in range(blocks):
-                at = pl.multiple_of((h * blocks + j) * pair + l * rank, rank)
-                part[pl.ds(at, rank), :] = value[:, j * LANES : (j + 1) * LANES]
+                part[group, block_of(h, j, l), :] = value[:, j * LANES : (j + 1) * LANES]
 
     waits = []
 
-    def reduce_scatter(source, near_buf, sums, far_buf, phase, mid, mid2):
-        size = source.shape[0] // 2
-        share = size // q
-        mine = pl.ds(pl.multiple_of(c * size, size), size)
-        theirs = pl.ds(pl.multiple_of(o * size, size), size)
-        core = send(source.at[theirs], near_buf, core_s.at[phase], core_r.at[phase], partner)
-        mid()
+    def halves(buf):
+        size = buf.shape[0] // 2
+        return [pl.ds(pl.multiple_of(h * size, size), size) for h in (c, o)]
+
+    def core_start(source, near_buf, phase):
+        theirs = halves(source)[1]
+        copy = send(source.at[theirs], near_buf, core_s.at[phase], core_r.at[phase], partner)
+        waits.append(copy)
+        return copy
+
+    def scatter_start(core, source, near_buf, sums, far_buf, phase):
+        mine = halves(source)[0]
+        share = sums.shape[0] // q
         core.wait_recv()
         sums[...] = source[mine, :] + near_buf[...]
         copies = []
@@ -132,12 +142,15 @@
                 send(sums.at[to], far_buf.at[d - 1], rs_s.at[phase, d - 1],
                      rs_r.at[phase, d - 1], chip(d))
             )
-        mid2()
+        waits.extend(copies)
+        return copies
+
+    def scatter_end(copies, sums, far_buf):
+        share = sums.shape[0] // q
         total = sums[pl.ds(pl.multiple_of(k * share, share), share), :]
         for d in range(1, q):
             copies[d - 1].wait_recv()
             total = total + far_buf[d - 1]
-        waits.extend([core] + copies)
         return total
 
     def gather_start(buf, phase):
@@ -166,37 +179,44 @@
             copy.wait_recv()
         waits.extend(copies + forwards)
 
-    part_of(o, 0)
-    pl.semaphore_wait(barrier, len(peers))
-    share = reduce_scatter(
-        part, from_core, summed, arrived, 0, lambda: part_of(c, 1), lambda: None
-    )
-    size = part.shape[0] // n
-    left[pl.ds(pl.multiple_of((c * q + k) * size, size), size), :] = share
-    copies, forwards = gather_start(left, 0)
-    gather_pass(left, 0, copies, forwards)
+    scatters = []
+    for group in range(groups):
+        part_of(o, 0, group)
+        if group == 0:
+            pl.semaphore_wait(barrier, len(peers))
+        core = core_start(part.at[group], from_core.at[group], group)
+        part_of(c, 1, group)
+        scatters.append(
+            scatter_start(core, part.at[group], from_core.at[group], summed.at[group],
+                          arrived.at[group], group)
+        )
+    gathers = []
+    size = part.shape[1] // n
+    for group in range(groups):
+        share = scatter_end(scatters[group], summed.at[group], arrived.at[group])
+        left[group, pl.ds(pl.multiple_of((c * q + k) * size, size), size), :] = share
+        gathers.append(gather_start(left.at[group], group))
+
+    def left_of(h, l):
+        return jnp.concatenate(
+            [left[l // deep, block_of(h, j, l), :] for j in range(blocks)], axis=1
+        )
 
     def lefts(h):
-        return [
-            jnp.concatenate(
-                [
-                    left[pl.ds(pl.multiple_of((h * blocks + j) * pair + l * rank, rank), rank), :]
-                    for j in range(blocks)
-                ],
-                axis=1,
-            )
-            for l in range(layers)
-        ]
-
-    def right_of(h):
-        return [
-            jnp.dot(value.astype(BF16), g[l, rows_of(h), :], preferred_element_type=F32)
-            for l, value in enumerate(lefts(h))
-        ]
-
-    own_right = right_of(c)
-    gather_end(copies, forwards)
-    own_right = [a + v for a, v in zip(own_right, right_of(o))]
+        return [left_of(h, l) for l in range(layers)]
+
+    def right_of(h, l):
+        return jnp.dot(
+            left_of(h, l).astype(BF16), g[l, rows_of(h), :], preferred_element_type=F32
+        )
+
+    own_right = []
+    for group in range(groups):
+        gather_pass(left.at[group], group, *gathers[group])
+        members = range(group * deep, (group + 1) * deep)
+        firsts = [right_of(c, l) for l in members]
+        gather_end(*gathers[group])
+        own_right.extend(a + right_of(o, l) for a, l in zip(firsts, members))
     if layers * wc < LANES:
         r_part[...] = jnp.zeros_like(r_part)
     for idx in range(n):
@@ -244,7 +264,11 @@
             inside = (lane >= l * rank) & (lane < (l + 1) * rank)
             inverses.append(jnp.where(inside, a, 0.0)[:, :pair])
 
-    total = reduce_scatter(r_part, r_core, r_sum, r_arrived, 1, make_gram, solve)
+    core = core_start(r_part, r_core, groups)
+    make_gram()
+    copies = scatter_start(core, r_part, r_core, r_sum, r_arrived, groups)
+    solve()
+    total = scatter_end(copies, r_sum, r_arrived)
     waits.extend(gram_copies)
     r_model[x] = total
     swaps = [
@@ -258,7 +282,7 @@
     for i in range(1, m):
         total = total + r_model[i]
     right[pl.ds(pl.multiple_of((c * q + k) * rank, rank), rank), :] = total
-    copies, forwards = gather_start(right, 1)
+    copies, forwards = gather_start(right, groups)
 
     mixed = jnp.dot(
         jnp.concatenate(inverses, axis=0),
@@ -283,7 +307,7 @@
             copy.start()
             stores.append(copy)
 
-    gather_pass(right, 1, copies, forwards)
+    gather_pass(right, groups, copies, forwards)
     gather_end(copies, forwards)
     squares = jnp.zeros((rank, LANES), F32)
     for pos in range(n):
@@ -333,6 +357,8 @@
     pair = layers * rank
     q = n // 2
     tall = rows // LANES * pair
+    groups = layers if tall // layers % (8 * n) == 0 else 1
+    deep = tall // groups
     dma = pltpu.SemaphoreType.DMA
     vmem = pltpu.VMEM
     outs = pl.pallas_call(
@@ -350,11 +376,11 @@
             vmem(layer_weights.shape, F32),
             vmem(momentum.shape, F32),
             vmem((layers, 4 * rank, rows), BF16),
-            vmem((tall, LANES), F32),
-            vmem((tall // 2, LANES), F32),
-            vmem((tall // 2, LANES), F32),
-            vmem((q - 1, tall // n, LANES), F32),
-            vmem((tall, LANES), F32),
+            vmem((groups, deep, LANES), F32),
+            vmem((groups, deep // 2, LANES), F32),
+            vmem((groups, deep // 2, LANES), F32),
+            vmem((groups, q - 1, deep // n, LANES), F32),
+            vmem((groups, deep, LANES), F32),
             vmem((n * rank, LANES), F32),
             vmem((q * rank, LANES), F32),
             vmem((q * rank, LANES), F32),
@@ -364,10 +390,10 @@
             vmem((m, pair, LANES), F32),
             vmem(last_basis.shape, F32),
             dma((3 + 2 * layers,)),
-            dma((2,)), dma((2,)),
-            dma((2, q - 1)), dma((2, q - 1)),
-            dma((2, q - 1)), dma((2, q - 1)),
-            dma((2, q)), dma((2, q)),
+            dma((groups + 1,)), dma((groups + 1,)),
+            dma((groups + 1, q - 1)), dma((groups + 1, q - 1)),
+            dma((groups + 1, q - 1)), dma((groups + 1, q - 1)),
+            dma((groups + 1, q)), dma((groups + 1, q)),
             dma((2, m - 1)), dma((2, m - 1)),
         ],
         compiler_params=pltpu.CompilerParams(

time: 42.6 us -> 42 us (0.986)
  Pallas kernels: 41.9 us -> 41.2 us
    pallas_call x1, Pallas kernels: 40.4 us -> 39.8 us  [shards(): pl.pallas_call(functools.partial(kernel, n, m), out_shape=(jax.ShapeDtype...]
where the time goes in v3:
time: 42 us; the launch traced here: 41.9 us
  Pallas kernels  41.2 us (98%)
  between operations  0.64 us (2%)
    pallas_call x1, Pallas kernels, shards(): pl.pallas_call(functools.partial(kernel, n, m), out_shape=(jax.ShapeDtype...  39.8 us
    pallas_call x1, Pallas kernels, shards(): pl.pallas_call(write_out, out_shape=tuple((jax.ShapeDtypeStruct(a.shape,...  1.43 us

profile of v3, /device:TPU:1, one launch (start us, length us, event | category | flops | bytes accessed | tf_op | source)
XLA Modules:
  0.0 41.9 jit_solution(2072859873698700709)
XLA Ops:
  0.6 39.8 %step.1 = (f32[2,64,2048]{2,1,0:T(8,128)S(1)}, f32[2,32,1024]{2,1,0:T(8,128)S(1)}, f32[2,64,2048]{2,1,0:T(8,128)S(1)}) custom-call(bf16[1,2,2048,1024]{3,2,1,0:T(8,128)(2,1)} %grads.1, f32[2,32,1024]{2,1,0:T(8,128)} %bitcast.8, f32[2,64,2048]{2,1,0:T(8,128)} %bitcast.6, f32[2,64,2048]{2,1,0:T(8,128)} %bitcast.7), custom_call_target="tpu_custom_call" | custom-call | tf_op jit(solution)/shard_map/step/pallas_call | solution.py:364
  40.4 1.4 %write_out.1 = (f32[2,64,2048]{2,1,0:T(8,128)}, f32[2,32,1024]{2,1,0:T(8,128)}, f32[2,64,2048]{2,1,0:T(8,128)}) custom-call(f32[2,64,2048]{2,1,0:T(8,128)S(1)} %get-tuple-element.9.refs_0_, f32[2,32,1024]{2,1,0:T(8,128)S(1)} %get-tuple-element.10.refs_1_, f32[2,64,2048]{2,1,0:T(8,128)S(1)} %get-tuple-element.11.refs_2_), custom_call_target="tpu_custom_call" | custom-call | tf_op jit(solution)/shard_map/write_out/pallas_call | solution.py:409

commit v4 on v3

--- a/solution.py
+++ b/solution.py
@@ -74,6 +74,14 @@
     def chip(d):
         return {"replica": 2 * near(d) + c}
 
+    wide = max(e for e in range(1, q + 1) if q % e == 0 and e * e <= q)
+    far = q // wide
+    row, col = k // wide, lax.rem(k, wide)
+
+    def cell(a, e):
+        at = lax.rem(row + a, far) * wide + lax.rem(col + e, wide)
+        return {"replica": 2 * at + c}
+
     def other(d):
         return {"model": lax.rem(x + d, m)}
 
@@ -174,10 +182,44 @@
                 send(buf.at[at], buf.at[at], fwd_s.at[phase, d], fwd_r.at[phase, d], partner)
             )
 
+    def spread_start(buf, phase):
+        share = buf.shape[0] // n
+        own = pl.ds(pl.multiple_of((c * q + k) * share, share), share)
+        copies = {}
+        for a, e in [(a, 0) for a in range(1, far)] + [(0, e) for e in range(1, wide)]:
+            copies[a, e] = send(
+                buf.at[own], buf.at[own], ag_s.at[phase, a * wide + e - 1],
+                ag_r.at[phase, a * wide + e - 1], cell(a, e),
+            )
+        forwards = [
+            send(buf.at[own], buf.at[own], fwd_s.at[phase, 0], fwd_r.at[phase, 0], partner)
+        ]
+        return copies, forwards
+
+    def spread_pass(buf, phase, copies, forwards):
+        share = buf.shape[0] // n
+        order = [(a, 0) for a in range(1, far)]
+        order += [(a, e) for a in range(far) for e in range(1, wide)]
+        for a, e in order:
+            copies[a, e].wait_recv()
+            at = (c * q + lax.rem(row + far - a, far) * wide + lax.rem(col + wide - e, wide)) * share
+            at = pl.ds(pl.multiple_of(at, share), share)
+            if e == 0:
+                for f in range(1, wide):
+                    copies[a, f] = send(
+                        buf.at[at], buf.at[at], ag_s.at[phase, a * wide + f - 1],
+                        ag_r.at[phase, a * wide + f - 1], cell(0, f),
+                    )
+            forwards.append(
+                send(buf.at[at], buf.at[at], fwd_s.at[phase, a * wide + e],
+                     fwd_r.at[phase, a * wide + e], partner)
+            )
+
     def gather_end(copies, forwards):
         for copy in forwards:
             copy.wait_recv()
-        waits.extend(copies + forwards)
+        waits.extend(list(copies.values()) if isinstance(copies, dict) else copies)
+        waits.extend(forwards)
 
     scatters = []
     for group in range(groups):
@@ -195,7 +237,7 @@
     for group in range(groups):
         share = scatter_end(scatters[group], summed.at[group], arrived.at[group])
         left[group, pl.ds(pl.multiple_of((c * q + k) * size, size), size), :] = share
-        gathers.append(gather_start(left.at[group], group))
+        gathers.append(spread_start(left.at[group], group))
 
     def left_of(h, l):
         return jnp.concatenate(
@@ -212,7 +254,7 @@
 
     own_right = []
     for group in range(groups):
-        gather_pass(left.at[group], group, *gathers[group])
+        spread_pass(left.at[group], group, *gathers[group])
         members = range(group * deep, (group + 1) * deep)
         firsts = [right_of(c, l) for l in members]
         gather_end(*gathers[group])

time: 42 us -> 44 us (1.048)
  Pallas kernels: 41.2 us -> 43.2 us
    pallas_call x1, Pallas kernels: 39.8 us -> 41.8 us  [shards(): pl.pallas_call(functools.partial(kernel, n, m), out_shape=(jax.ShapeDtype...]
where the time goes in v4:
time: 44 us; the launch traced here: 43.8 us
  Pallas kernels  43.2 us (98%)
  between operations  0.64 us (1%)
    pallas_call x1, Pallas kernels, shards(): pl.pallas_call(functools.partial(kernel, n, m), out_shape=(jax.ShapeDtype...  41.8 us
    pallas_call x1, Pallas kernels, shards(): pl.pallas_call(write_out, out_shape=tuple((jax.ShapeDtypeStruct(a.shape,...  1.43 us

profile of v4, /device:TPU:1, one launch (start us, length us, event | category | flops | bytes accessed | tf_op | source)
XLA Modules:
  0.0 43.8 jit_solution(8130908555156220650)
XLA Ops:
  0.6 41.8 %step.1 = (f32[2,64,2048]{2,1,0:T(8,128)S(1)}, f32[2,32,1024]{2,1,0:T(8,128)S(1)}, f32[2,64,2048]{2,1,0:T(8,128)S(1)}) custom-call(bf16[1,2,2048,1024]{3,2,1,0:T(8,128)(2,1)} %grads.1, f32[2,32,1024]{2,1,0:T(8,128)} %bitcast.8, f32[2,64,2048]{2,1,0:T(8,128)} %bitcast.6, f32[2,64,2048]{2,1,0:T(8,128)} %bitcast.7), custom_call_target="tpu_custom_call" | custom-call | tf_op jit(solution)/shard_map/step/pallas_call | solution.py:406
  42.4 1.4 %write_out.1 = (f32[2,64,2048]{2,1,0:T(8,128)}, f32[2,32,1024]{2,1,0:T(8,128)}, f32[2,64,2048]{2,1,0:T(8,128)}) custom-call(f32[2,64,2048]{2,1,0:T(8,128)S(1)} %get-tuple-element.9.refs_0_, f32[2,32,1024]{2,1,0:T(8,128)S(1)} %get-tuple-element.10.refs_1_, f32[2,64,2048]{2,1,0:T(8,128)S(1)} %get-tuple-element.11.refs_2_), custom_call_target="tpu_custom_call" | custom-call | tf_op jit(solution)/shard_map/write_out/pallas_call | solution.py:451
